TPU v7x, 32 devices: a whole 2x2x4 slice. The times are simulated.
32 devices in a mesh: owner: 4 (over y, core), rows: 8 (over z, x).
Axes of the slice: x: 2, y: 2, z: 4, core: 2. Of those that a mesh axis runs over, the one named last changes fastest.
Arguments:
- train_gate: float32 [64, 2048, 1024], P('owner', 'rows'), may hold values from -0.1875 to 0.1875
- other_gate: bfloat16 [64, 2048, 1024], P('owner', 'rows'), may hold values from -0.0625 to 0.0625
- train_up: float32 [64, 2048, 1024], P('owner', 'rows'), may hold values from -0.1875 to 0.1875
- other_up: bfloat16 [64, 2048, 1024], P('owner', 'rows'), may hold values from -0.0625 to 0.0625
- train_down: float32 [64, 1024, 2048], P('owner', None, 'rows'), may hold values from -0.25 to 0.25
- other_down: bfloat16 [64, 1024, 2048], P('owner', None, 'rows'), may hold values from -0.09375 to 0.09375
- router_weight: float32 [2048, 64], P('rows', 'owner'), may hold values from -0.125 to 0.125
- router_gain: float32 [2048], P('rows'), may hold values from 0.25 to 1.75
Outputs:
- ready_gate: bfloat16 [64, 2048, 1024], P('owner', None, 'rows')
- ready_up: bfloat16 [64, 2048, 1024], P('owner', None, 'rows')
- ready_down: bfloat16 [64, 1024, 2048], P('owner', 'rows')
- scale_gate: float32 [64, 1024], P('owner', 'rows')
- scale_up: float32 [64, 1024], P('owner', 'rows')
- scale_down: float32 [64, 1024], P('owner', 'rows')
- serve_router: bfloat16 [2048, 64], replicated
All inputs are finite; a program needn't handle non-finite values. Where the computation divides by a largest or mean magnitude, that divisor is 1e-20 or more.
Results may differ from a plain program's by a relative error of at most 0.001.
Values may be sent and summed in bfloat16 or wider, within the bound.
A program may use at most 192 MiB of HBM per device.

v0:
```python
import jax
import jax.numpy as jnp
from jax import lax
from jax.sharding import PartitionSpec as P


def shards(
    train_gate, other_gate, train_up, other_up, train_down, other_down, router_weight, router_gain
):
    latest_gate = train_gate + other_gate.astype(jnp.float32)
    latest_up = train_up + other_up.astype(jnp.float32)
    latest_down = train_down + other_down.astype(jnp.float32)
    scale_gate, scale_up, scale_down = lax.pmax(
        (
            jnp.max(jnp.abs(latest_gate), axis=1),
            jnp.max(jnp.abs(latest_up), axis=1),
            jnp.max(jnp.abs(latest_down), axis=2),
        ),
        "rows",
    )
    narrow_gate, narrow_up, narrow_down = (
        (latest_gate / jnp.expand_dims(scale_gate, 1)).astype(jnp.bfloat16),
        (latest_up / jnp.expand_dims(scale_up, 1)).astype(jnp.bfloat16),
        (latest_down / jnp.expand_dims(scale_down, 2)).astype(jnp.bfloat16),
    )
    ready_gate, ready_up = (
        lax.all_to_all(narrow_gate, "rows", split_axis=2, concat_axis=1, tiled=True),
        lax.all_to_all(narrow_up, "rows", split_axis=2, concat_axis=1, tiled=True),
    )
    ready_down = lax.all_to_all(narrow_down, "rows", split_axis=1, concat_axis=2, tiled=True)
    scale_gate = lax.dynamic_slice_in_dim(
        scale_gate, lax.axis_index("rows") * ready_gate.shape[2], ready_gate.shape[2], axis=1
    )
    scale_up = lax.dynamic_slice_in_dim(
        scale_up, lax.axis_index("rows") * ready_up.shape[2], ready_up.shape[2], axis=1
    )
    scale_down = lax.dynamic_slice_in_dim(
        scale_down, lax.axis_index("rows") * ready_down.shape[1], ready_down.shape[1], axis=1
    )
    part_router = (router_weight * router_gain[:, None]).astype(jnp.bfloat16)
    row_router = lax.all_gather(part_router, "rows", axis=0, tiled=True)
    serve_router = lax.all_gather(row_router, "owner", axis=1, tiled=True)
    return (ready_gate, ready_up, ready_down, scale_gate, scale_up, scale_down, serve_router)


def solution(mesh):
    placed = (
        P("owner", "rows", None),
        P("owner", "rows", None),
        P("owner", "rows", None),
        P("owner", "rows", None),
        P("owner", None, "rows"),
        P("owner", None, "rows"),
        P("rows", "owner"),
        P("rows"),
    )
    return jax.shard_map(
        shards,
        mesh=mesh,
        in_specs=placed,
        out_specs=(
            P("owner", None, "rows"),
            P("owner", None, "rows"),
            P("owner", "rows", None),
            P("owner", "rows"),
            P("owner", "rows"),
            P("owner", "rows"),
            P(),
        ),
        check_vma=False,
    )
```

profile of v0, /device:TPU:0, one launch (start us, length us, event | category | flops | bytes accessed | tf_op | source)
XLA Modules:
  0.0 877.2 jit_solution(6322543164802641597)
XLA Ops:
  7.2 0.0 all-reduce.3.cloned.1.call-start
  7.2 17.6 %copy.34 = f32[16,256,1024]{1,0,2:T(8,128)} copy(f32[16,256,1024]{2,1,0:T(8,128)} %param.10) | data formatting | bytes 33554432 | tf_op args[2]
  24.8 12.5 %copy.33 = bf16[16,256,1024]{1,0,2:T(8,128)(2,1)} copy(bf16[16,256,1024]{2,1,0:T(8,128)(2,1)} %param.11) | data formatting | bytes 16777216 | tf_op args[3]
  37.3 17.6 %copy.31 = f32[16,256,1024]{1,0,2:T(8,128)} copy(f32[16,256,1024]{2,1,0:T(8,128)} %param.8) | data formatting | bytes 33554432 | tf_op args[0]
  54.9 12.5 %copy.30 = bf16[16,256,1024]{1,0,2:T(8,128)(2,1)} copy(bf16[16,256,1024]{2,1,0:T(8,128)(2,1)} %param.9) | data formatting | bytes 16777216 | tf_op args[1]
  67.4 0.0 copy-start
  67.4 0.0 copy-start.1
  67.4 0.0 slice-start
  67.4 11.1 %abs_reduce_fusion.1 = f32[16,1024]{0,1:T(8,128)} fusion(f32[16,256,1024]{1,0,2:T(8,128)} %copy.34, bf16[16,256,1024]{1,0,2:T(8,128)(2,1)} %copy.33), kind=kLoop, calls=%fused_computation.4 | loop fusion | flops 16760832 | bytes 25231360 | tf_op jit(solution)/shard_map/reduce_max | solution.py:16
  78.5 2.1 copy-done
  80.6 2.4 copy-done.1
  83.0 0.0 slice-start.1
  83.0 4.3 abs_reduce_fusion.2
  87.3 0.0 slice-done
  87.3 0.0 slice-done.1
  87.3 29.3 %abs_reduce_fusion = f32[16,1024]{0,1:T(8,128)} fusion(f32[16,1024,256]{2,1,0:T(8,128)} %param.12, bf16[16,1024,256]{2,1,0:T(8,128)(2,1)S(1)} %bitcast.14), kind=kLoop, calls=%fused_computation.2 | loop fusion | flops 16760832 | bytes 25231360 | tf_op jit(solution)/shard_map/reduce_max | solution.py:17
  116.5 0.0 all-reduce.3.cloned.1.call-update
  116.6 92.5 %all-reduce.3.cloned.1.call-done = (f32[16,1024]{0,1:T(8,128)}, f32[16,1024]{0,1:T(8,128)}, f32[16,1024]{0,1:T(8,128)}) async-done(((f32[16,1024]{0,1:T(8,128)}, f32[16,1024]{0,1:T(8,128)}, f32[16,1024]{0,1:T(8,128)}), (f32[16,1024]{0,1:T(8,128)}, f32[16,1024]{0,1:T(8,128)}, f32[16,1024]{0,1:T(8,128)})) %all-reduce.3.cloned.1.call-update) | async-done | bytes 196624 | tf_op jit(solution)/shard_map/pmax | solution.py:13
  209.0 20.5 %divide_convert_fusion.1 = (bf16[16,256,1024]{1,0,2:T(8,128)(2,1)}, bf16[16,256,1024]{1,0,2:T(8,128)(2,1)S(1)}) fusion(f32[16,256,1024]{1,0,2:T(8,128)} %copy.34, bf16[16,256,1024]{1,0,2:T(8,128)(2,1)} %copy.33, f32[16,1024]{0,1:T(8,128)} %get-tuple-element.15, f32[16,1024]{0,1:T(8,128)} %get-tuple-element.14, f32[16,256,1024]{1,0,2:T(8,128)} %copy.31, ...), kind=kLoop, calls=%fused_computation.3 | loop fusion | flops 33554432 | bytes 67239936 | tf_op jit(solution)/shard_map/convert_element_type | solution.py:23
  229.6 0.0 copy-start.2
  229.6 187.0 %all_to_all.54 = bf16[16,256,1024]{1,0,2:T(8,128)(2,1)} all-to-all(bf16[16,256,1024]{1,0,2:T(8,128)(2,1)S(1)} %get-tuple-element.18), channel_id=1, replica_groups=mesh['owner'=4,'rows'=8] {'rows'}, dimensions={2} | all-to-all | bytes 16777216 | tf_op jit(solution)/shard_map/all_to_all | solution.py:27
  416.6 4.9 all-to-all-start.1
  421.5 0.0 copy-done.2
  421.5 23.8 %divide_convert_fusion = bf16[16,1024,256]{2,0,1:T(8,128)(2,1)} fusion(f32[16,1024,256]{2,1,0:T(8,128)} %param.12, f32[16,1024]{0,1:T(8,128)S(1)} %copy-done.2, bf16[16,1024,256]{2,1,0:T(8,128)(2,1)} %param.13), kind=kLoop, calls=%fused_computation.1 | loop fusion | flops 16777216 | bytes 33619968 | tf_op jit(solution)/shard_map/convert_element_type | solution.py:24
  445.3 0.0 copy-start.3
  445.3 0.0 copy-start.4
  445.3 158.3 %all-to-all-done.1 = bf16[16,256,1024]{1,0,2:T(8,128)(2,1)} async-done(((bf16[16,256,1024]{1,0,2:T(8,128)(2,1)}), bf16[16,256,1024]{1,0,2:T(8,128)(2,1)}, u32[]{:S(2)}, u32[]{:S(2)}) %all-to-all-start.1) | async-done | bytes 8388640 | tf_op jit(solution)/shard_map/all_to_all | solution.py:28
  603.6 5.0 all-to-all-start.2
  608.6 0.0 copy-done.3
  608.7 0.0 copy-done.4
  608.7 201.9 %all_gather.6 = bf16[2048,16]{0,1:T(8,128)(2,1)S(1)} all-gather(bf16[256,16]{0,1:T(8,128)(2,1)S(1)} %multiply_convert_fusion), channel_id=1, replica_groups=mesh['owner'=4,'rows'=8] {'rows'}, dimensions={0}, use_global_device_ids=true | all-gather | bytes 73728 | tf_op jit(solution)/shard_map/all_gather | solution.py:41
  810.6 6.0 all_gather.7
  816.5 0.8 constant_dynamic-slice_fusion
  817.4 0.7 copy.40
  818.1 0.7 copy.41
  818.7 0.8 constant_dynamic-slice_fusion.2
  819.6 0.7 copy.39
  820.2 12.3 %copy.32 = bf16[16,8,256,128]{3,2,1,0:T(8,128)(2,1)} copy(bf16[16,8,256,128]{2,0,3,1:T(8,128)(2,1)} %bitcast.15) | data formatting | bytes 16777216 | tf_op jit(solution)/shard_map/all_to_all | solution.py:27
  832.5 12.3 %copy.35 = bf16[16,8,256,128]{3,2,1,0:T(8,128)(2,1)} copy(bf16[16,8,256,128]{2,0,3,1:T(8,128)(2,1)} %bitcast.4) | data formatting | bytes 16777216 | tf_op jit(solution)/shard_map/all_to_all | solution.py:28
  844.8 0.0 all-to-all-done.2
  844.8 11.4 %copy.38 = bf16[16,128,8,256]{3,2,1,0:T(8,128)(2,1)} copy(bf16[16,128,8,256]{3,0,1,2:T(8,128)(2,1)} %bitcast.7) | data formatting | bytes 16777216 | tf_op jit(solution)/shard_map/all_to_all | solution.py:30
  856.2 13.4 %all_to_all.50 = bf16[16,128,2048]{2,1,0:T(8,128)(2,1)} reshape(bf16[16,128,8,256]{3,2,1,0:T(8,128)(2,1)} %copy.38) | data formatting | bytes 16777216 | tf_op jit(solution)/shard_map/all_to_all | solution.py:30
  869.6 0.7 copy.53
  (2 shorter events, 0.0 us)
Async XLA Ops:
  7.2 201.9 %all-reduce.3.cloned.1.call-start = ((), (), s32[]{:S(2)}) async-start(), calls=%async_computation.3 | async-start | bytes 3145728 | tf_op jit(solution)/shard_map/pmax | solution.py:13
  67.4 13.2 %copy-start = (f32[16,256,1024]{1,0,2:T(8,128)S(1)}, f32[16,256,1024]{1,0,2:T(8,128)}, u32[]{:S(2)}) copy-start(f32[16,256,1024]{1,0,2:T(8,128)} %copy.31) | copy-start | bytes 50331652
  67.4 15.6 %copy-start.1 = (bf16[16,256,1024]{1,0,2:T(8,128)(2,1)S(1)}, bf16[16,256,1024]{1,0,2:T(8,128)(2,1)}, u32[]{:S(2)}) copy-start(bf16[16,256,1024]{1,0,2:T(8,128)(2,1)} %copy.30) | copy-start | bytes 25165828
  67.4 19.9 %slice-start = ((s8[8388608]{0:T(1024)(128)(4,1)}), s8[4194304]{0:T(1024)(128)(4,1)S(1)}, s32[]{:S(2)}) async-start(s8[8388608]{0:T(1024)(128)(4,1)} %bitcast.13), calls=%async_computation.4 | async-start | bytes 8388608
  83.0 4.3 slice-start.1
  229.6 192.0 %copy-start.2 = (f32[16,1024]{0,1:T(8,128)S(1)}, f32[16,1024]{0,1:T(8,128)}, u32[]{:S(2)}) copy-start(f32[16,1024]{0,1:T(8,128)} %get-tuple-element.16) | copy-start | bytes 196612
  416.6 187.0 %all-to-all-start.1 = ((bf16[16,256,1024]{1,0,2:T(8,128)(2,1)}), bf16[16,256,1024]{1,0,2:T(8,128)(2,1)}, u32[]{:S(2)}, u32[]{:S(2)}) async-start(bf16[16,256,1024]{1,0,2:T(8,128)(2,1)} %get-tuple-element.17), calls=%async_computation.1 | async-start | bytes 16777216 | tf_op jit(solution)/shard_map/all_to_all | solution.py:28
  445.3 163.3 %copy-start.3 = (f32[256,16]{0,1:T(8,128)S(1)}, f32[256,16]{0,1:T(8,128)}, u32[]{:S(2)}) copy-start(f32[256,16]{0,1:T(8,128)} %param.14) | copy-start | bytes 49156
  445.3 163.3 %copy-start.4 = (f32[256]{0:T(256)S(1)}, f32[256]{0:T(256)}, u32[]{:S(2)}) copy-start(f32[256]{0:T(256)} %param.15) | copy-start | bytes 3076
  603.6 241.2 %all-to-all-start.2 = ((bf16[16,1024,256]{2,0,1:T(8,128)(2,1)}), bf16[16,1024,256]{2,0,1:T(8,128)(2,1)}, u32[]{:S(2)}, u32[]{:S(2)}) async-start(bf16[16,1024,256]{2,0,1:T(8,128)(2,1)} %divide_convert_fusion), calls=%async_computation.2 | async-start | bytes 16777216 | tf_op jit(solution)/shard_map/all_to_all | solution.py:30
Sparse Core Ops, SparseCore 0:
  116.7 92.2 all-reduce.2
where the time goes:
time: 880 us; the launch traced here: 877 us
  blocking collectives  395 us (45%)
  waiting for transfers between devices  251 us (29%)
  local copies, waits for them, and re-layouts  118 us (13%)
  other arithmetic  88.9 us (10%)
  between operations  14.1 us (2%)
  starting transfers between devices  10 us (1%)
    all_gather x1, blocking collectives, shards(): row_router = lax.all_gather(part_router, 'rows', axis=0, tiled=True)  202 us
    all_to_all x1, blocking collectives, shards(): lax.all_to_all(narrow_gate, 'rows', split_axis=2, concat_axis=1, tiled=True)  187 us
    all_to_all x1, waiting for transfers between devices, shards(): lax.all_to_all(narrow_up, 'rows', split_axis=2, concat_axis=1, tiled=True)  158 us
    pmax x1, waiting for transfers between devices, shards(): lax.pmax((jnp.max(jnp.abs(latest_gate), axis=1), jnp.max(jnp.abs(latest_u...  92.5 us
    unnamed x22, local copies, waits for them, and re-layouts  67.4 us
    reduce_max x1, other arithmetic, shards(): jnp.max(jnp.abs(latest_down), axis=2)  29.3 us
    all_to_all x2, local copies, waits for them, and re-layouts, shards(): lax.all_to_all(narrow_down, 'rows', split_axis=1, concat_axis=2, tiled=True)  24.8 us
    convert_element_type x1, other arithmetic, shards(): (latest_down / jnp.expand_dims(scale_down, 2)).astype(jnp.bfloat16)  23.8 us
  transfers between devices with their start and end apart: 3, of which 2 were waited for; matrix products, arithmetic and copies ran while one was open for 6% of the time, Pallas kernels for 0%

commit v1 on v0

--- a/solution.py
+++ b/solution.py
@@ -38,7 +38,9 @@
         scale_down, lax.axis_index("rows") * ready_down.shape[1], ready_down.shape[1], axis=1
     )
     part_router = (router_weight * router_gain[:, None]).astype(jnp.bfloat16)
-    row_router = lax.all_gather(part_router, "rows", axis=0, tiled=True)
+    row_router = jnp.concatenate(
+        lax.all_to_all(jnp.stack([part_router] * lax.axis_size("rows")), "rows", 0, 0), axis=0
+    )
     serve_router = lax.all_gather(row_router, "owner", axis=1, tiled=True)
     return (ready_gate, ready_up, ready_down, scale_gate, scale_up, scale_down, serve_router)
 

time: 880 us -> 832 us (0.945)
  blocking collectives: 395 us -> 195 us
  waiting for transfers between devices: 251 us -> 392 us
    all_gather x1 -> x0, blocking collectives: 202 us -> none  [shards(): row_router = lax.all_gather(part_router, 'rows', axis=0, tiled=True)]
    all_to_all x1, waiting for transfers between devices: 0.01 us -> 148 us  [shards(): lax.all_to_all(narrow_down, 'rows', split_axis=1, concat_axis=2, tiled=True)]
  transfers between devices with their start and end apart: 3 -> 4, of which waited for: 2 -> 3; matrix products, arithmetic and copies ran while one was open for 6% -> 9% of each run, Pallas kernels for 0% -> 0%
where the time goes in v1:
time: 832 us; the launch traced here: 830 us
  waiting for transfers between devices  392 us (47%)
  blocking collectives  195 us (23%)
  local copies, waits for them, and re-layouts  119 us (14%)
  other arithmetic  91.9 us (11%)
  starting transfers between devices  17.3 us (2%)
  between operations  14.1 us (2%)
    all_to_all x1, blocking collectives, shards(): lax.all_to_all(narrow_gate, 'rows', split_axis=2, concat_axis=1, tiled=True)  189 us
    all_to_all x1, waiting for transfers between devices, shards(): lax.all_to_all(narrow_up, 'rows', split_axis=2, concat_axis=1, tiled=True)  159 us
    all_to_all x1, waiting for transfers between devices, shards(): lax.all_to_all(narrow_down, 'rows', split_axis=1, concat_axis=2, tiled=True)  148 us
    pmax x1, waiting for transfers between devices, shards(): lax.pmax((jnp.max(jnp.abs(latest_gate), axis=1), jnp.max(jnp.abs(latest_u...  85.9 us
    unnamed x22, local copies, waits for them, and re-layouts  67.4 us
    reduce_max x1, other arithmetic, shards(): jnp.max(jnp.abs(latest_down), axis=2)  29.3 us
    all_to_all x2, local copies, waits for them, and re-layouts, shards(): lax.all_to_all(narrow_down, 'rows', split_axis=1, concat_axis=2, tiled=True)  24.8 us
    convert_element_type x1, other arithmetic, shards(): (latest_down / jnp.expand_dims(scale_down, 2)).astype(jnp.bfloat16)  23.8 us
  transfers between devices with their start and end apart: 4, of which 3 were waited for; matrix products, arithmetic and copies ran while one was open for 9% of the time, Pallas kernels for 0%

profile of v1, /device:TPU:0, one launch (start us, length us, event | category | flops | bytes accessed | tf_op | source)
XLA Modules:
  0.0 829.8 jit_solution(11450437637752484735)
XLA Ops:
  7.2 0.0 all-reduce.3.cloned.1.call-start
  7.2 17.6 %copy.47 = f32[16,256,1024]{1,0,2:T(8,128)} copy(f32[16,256,1024]{2,1,0:T(8,128)} %param.10) | data formatting | bytes 33554432 | tf_op args[2]
  24.8 12.5 %copy.46 = bf16[16,256,1024]{1,0,2:T(8,128)(2,1)} copy(bf16[16,256,1024]{2,1,0:T(8,128)(2,1)} %param.11) | data formatting | bytes 16777216 | tf_op args[3]
  37.3 17.6 %copy.44 = f32[16,256,1024]{1,0,2:T(8,128)} copy(f32[16,256,1024]{2,1,0:T(8,128)} %param.8) | data formatting | bytes 33554432 | tf_op args[0]
  54.9 12.5 %copy.43 = bf16[16,256,1024]{1,0,2:T(8,128)(2,1)} copy(bf16[16,256,1024]{2,1,0:T(8,128)(2,1)} %param.9) | data formatting | bytes 16777216 | tf_op args[1]
  67.4 0.0 copy-start
  67.4 0.0 copy-start.1
  67.4 0.0 slice-start
  67.4 11.1 %abs_reduce_fusion.1 = f32[16,1024]{0,1:T(8,128)} fusion(f32[16,256,1024]{1,0,2:T(8,128)} %copy.47, bf16[16,256,1024]{1,0,2:T(8,128)(2,1)} %copy.46), kind=kLoop, calls=%fused_computation.4 | loop fusion | flops 16760832 | bytes 25231360 | tf_op jit(solution)/shard_map/reduce_max | solution.py:16
  78.5 2.1 copy-done
  80.6 2.4 copy-done.1
  83.0 0.0 slice-start.1
  83.0 4.3 abs_reduce_fusion.2
  87.2 0.0 slice-done
  87.2 0.0 slice-done.1
  87.2 0.0 copy-start.3
  87.2 0.0 copy-start.4
  87.2 29.3 %abs_reduce_fusion = f32[16,1024]{0,1:T(8,128)} fusion(f32[16,1024,256]{2,1,0:T(8,128)} %param.12, bf16[16,1024,256]{2,1,0:T(8,128)(2,1)S(1)} %bitcast.16), kind=kLoop, calls=%fused_computation.2 | loop fusion | flops 16760832 | bytes 25231360 | tf_op jit(solution)/shard_map/reduce_max | solution.py:17
  116.5 0.0 all-reduce.3.cloned.1.call-update
  116.6 0.0 copy-done.3
  116.6 0.0 copy-done.4
  116.6 0.6 stack.2
  117.2 7.3 all-to-all-start.3
  124.5 85.9 %all-reduce.3.cloned.1.call-done = (f32[16,1024]{0,1:T(8,128)}, f32[16,1024]{0,1:T(8,128)}, f32[16,1024]{0,1:T(8,128)}) async-done(((f32[16,1024]{0,1:T(8,128)}, f32[16,1024]{0,1:T(8,128)}, f32[16,1024]{0,1:T(8,128)}), (f32[16,1024]{0,1:T(8,128)}, f32[16,1024]{0,1:T(8,128)}, f32[16,1024]{0,1:T(8,128)})) %all-reduce.3.cloned.1.call-update) | async-done | bytes 196624 | tf_op jit(solution)/shard_map/pmax | solution.py:13
  210.4 23.5 %divide_convert_fusion.1 = (bf16[16,256,1024]{1,0,2:T(8,128)(2,1)}, bf16[16,256,1024]{1,0,2:T(8,128)(2,1)}) fusion(f32[16,256,1024]{1,0,2:T(8,128)} %copy.47, bf16[16,256,1024]{1,0,2:T(8,128)(2,1)} %copy.46, f32[16,1024]{0,1:T(8,128)} %get-tuple-element.15, f32[16,1024]{0,1:T(8,128)} %get-tuple-element.14, f32[16,256,1024]{1,0,2:T(8,128)} %copy.44, ...), kind=kLoop, calls=%fused_computation.3 | loop fusion | flops 33554432 | bytes 67239936 | tf_op jit(solution)/shard_map/convert_element_type | solution.py:23
  233.9 0.0 all-to-all-done.3
  233.9 0.0 copy-start.2
  233.9 189.3 %all_to_all.59 = bf16[16,256,1024]{1,0,2:T(8,128)(2,1)} all-to-all(bf16[16,256,1024]{1,0,2:T(8,128)(2,1)} %get-tuple-element.18), channel_id=1, replica_groups=mesh['owner'=4,'rows'=8] {'rows'}, dimensions={2} | all-to-all | bytes 16777216 | tf_op jit(solution)/shard_map/all_to_all | solution.py:27
  423.2 4.9 all-to-all-start.1
  428.2 0.0 copy-done.2
  428.2 23.8 %divide_convert_fusion = bf16[16,1024,256]{2,0,1:T(8,128)(2,1)} fusion(f32[16,1024,256]{2,1,0:T(8,128)} %param.12, f32[16,1024]{0,1:T(8,128)S(1)} %copy-done.2, bf16[16,1024,256]{2,1,0:T(8,128)(2,1)} %param.13), kind=kLoop, calls=%fused_computation.1 | loop fusion | flops 16777216 | bytes 33619968 | tf_op jit(solution)/shard_map/convert_element_type | solution.py:24
  451.9 158.6 %all-to-all-done.1 = bf16[16,256,1024]{1,0,2:T(8,128)(2,1)} async-done(((bf16[16,256,1024]{1,0,2:T(8,128)(2,1)}), bf16[16,256,1024]{1,0,2:T(8,128)(2,1)}, u32[]{:S(2)}, u32[]{:S(2)}) %all-to-all-start.1) | async-done | bytes 8388640 | tf_op jit(solution)/shard_map/all_to_all | solution.py:28
  610.5 5.0 all-to-all-start.2
  615.6 6.0 all_gather.3
  621.6 0.8 constant_dynamic-slice_fusion
  622.4 0.7 copy.54
  623.1 0.7 copy.55
  623.8 0.8 constant_dynamic-slice_fusion.2
  624.6 0.7 copy.53
  625.3 12.3 %copy.45 = bf16[16,8,256,128]{3,2,1,0:T(8,128)(2,1)} copy(bf16[16,8,256,128]{2,0,3,1:T(8,128)(2,1)} %bitcast.17) | data formatting | bytes 16777216 | tf_op jit(solution)/shard_map/all_to_all | solution.py:27
  637.6 12.3 %copy.48 = bf16[16,8,256,128]{3,2,1,0:T(8,128)(2,1)} copy(bf16[16,8,256,128]{2,0,3,1:T(8,128)(2,1)} %bitcast.4) | data formatting | bytes 16777216 | tf_op jit(solution)/shard_map/all_to_all | solution.py:28
  649.8 147.6 %all-to-all-done.2 = bf16[16,1024,256]{2,0,1:T(8,128)(2,1)} async-done(((bf16[16,1024,256]{2,0,1:T(8,128)(2,1)}), bf16[16,1024,256]{2,0,1:T(8,128)(2,1)}, u32[]{:S(2)}, u32[]{:S(2)}) %all-to-all-start.2) | async-done | bytes 8388640 | tf_op jit(solution)/shard_map/all_to_all | solution.py:30
  797.5 11.4 %copy.51 = bf16[16,128,8,256]{3,2,1,0:T(8,128)(2,1)} copy(bf16[16,128,8,256]{3,0,1,2:T(8,128)(2,1)} %bitcast.7) | data formatting | bytes 16777216 | tf_op jit(solution)/shard_map/all_to_all | solution.py:30
  808.9 13.4 %all_to_all.53 = bf16[16,128,2048]{2,1,0:T(8,128)(2,1)} reshape(bf16[16,128,8,256]{3,2,1,0:T(8,128)(2,1)} %copy.51) | data formatting | bytes 16777216 | tf_op jit(solution)/shard_map/all_to_all | solution.py:30
  822.3 0.7 copy.68
  (3 shorter events, 0.0 us)
Async XLA Ops:
  7.2 203.2 %all-reduce.3.cloned.1.call-start = ((), (), s32[]{:S(2)}) async-start(), calls=%async_computation.4 | async-start | bytes 3145728 | tf_op jit(solution)/shard_map/pmax | solution.py:13
  67.4 13.2 %copy-start = (f32[16,256,1024]{1,0,2:T(8,128)S(1)}, f32[16,256,1024]{1,0,2:T(8,128)}, u32[]{:S(2)}) copy-start(f32[16,256,1024]{1,0,2:T(8,128)} %copy.44) | copy-start | bytes 50331652
  67.4 15.6 %copy-start.1 = (bf16[16,256,1024]{1,0,2:T(8,128)(2,1)S(1)}, bf16[16,256,1024]{1,0,2:T(8,128)(2,1)}, u32[]{:S(2)}) copy-start(bf16[16,256,1024]{1,0,2:T(8,128)(2,1)} %copy.43) | copy-start | bytes 25165828
  67.4 19.9 %slice-start = ((s8[8388608]{0:T(1024)(128)(4,1)}), s8[4194304]{0:T(1024)(128)(4,1)S(1)}, s32[]{:S(2)}) async-start(s8[8388608]{0:T(1024)(128)(4,1)} %bitcast.15), calls=%async_computation.5 | async-start | bytes 8388608
  83.0 4.3 slice-start.1
  87.2 29.3 %copy-start.3 = (f32[256,16]{0,1:T(8,128)S(1)}, f32[256,16]{0,1:T(8,128)}, u32[]{:S(2)}) copy-start(f32[256,16]{0,1:T(8,128)} %param.14) | copy-start | bytes 49156
  87.2 29.3 %copy-start.4 = (f32[256]{0:T(256)S(1)}, f32[256]{0:T(256)}, u32[]{:S(2)}) copy-start(f32[256]{0:T(256)} %param.15) | copy-start | bytes 3076
  117.2 116.7 %all-to-all-start.3 = ((bf16[8,256,16]{1,2,0:T(8,128)(2,1)}), bf16[8,256,16]{1,2,0:T(8,128)(2,1)S(1)}, u32[]{:S(2)}, u32[]{:S(2)}) async-start(bf16[8,256,16]{1,2,0:T(8,128)(2,1)} %stack.2), calls=%async_computation.3 | async-start | bytes 131072 | tf_op jit(solution)/shard_map/all_to_all | solution.py:42
  233.9 194.3 %copy-start.2 = (f32[16,1024]{0,1:T(8,128)S(1)}, f32[16,1024]{0,1:T(8,128)}, u32[]{:S(2)}) copy-start(f32[16,1024]{0,1:T(8,128)} %get-tuple-element.16) | copy-start | bytes 196612
  423.2 187.3 %all-to-all-start.1 = ((bf16[16,256,1024]{1,0,2:T(8,128)(2,1)}), bf16[16,256,1024]{1,0,2:T(8,128)(2,1)}, u32[]{:S(2)}, u32[]{:S(2)}) async-start(bf16[16,256,1024]{1,0,2:T(8,128)(2,1)} %get-tuple-element.17), calls=%async_computation.1 | async-start | bytes 16777216 | tf_op jit(solution)/shard_map/all_to_all | solution.py:28
  610.5 187.0 %all-to-all-start.2 = ((bf16[16,1024,256]{2,0,1:T(8,128)(2,1)}), bf16[16,1024,256]{2,0,1:T(8,128)(2,1)}, u32[]{:S(2)}, u32[]{:S(2)}) async-start(bf16[16,1024,256]{2,0,1:T(8,128)(2,1)} %divide_convert_fusion), calls=%async_computation.2 | async-start | bytes 16777216 | tf_op jit(solution)/shard_map/all_to_all | solution.py:30
Sparse Core Ops, SparseCore 0:
  116.7 93.6 all-reduce.2
